TPU v7x, 32 devices: a whole 2x2x4 slice. The times are simulated.
32 devices in a mesh: dp: 4 (over y, x), vocab: 8 (over z, core).
Axes of the slice: x: 2, y: 2, z: 4, core: 2. Of those that a mesh axis runs over, the one named last changes fastest.
Arguments:
- token_ids: int32 [131072], P(('dp', 'vocab')), may hold values from 0 to 7679, as said below
- valid_counts: int32 [1024], P(('dp', 'vocab')), may hold values from 64 to 128
- grad_output: bfloat16 [131072, 768], P(('dp', 'vocab')), may hold values from -6 to 6
- pre_norm: bfloat16 [131072, 768], P(('dp', 'vocab')), may hold values from -6 to 6
- norm_gain: float32 [768], replicated, may hold values from 0.5 to 1.5
Outputs:
- grad_table: float32 [7680, 768], P('vocab')
Inputs may be any that keep to these rules, and one draw needn't show every extreme that they name: `token_ids`: of the 4096 positions of one device, at most 1024 have ids in any one range [k * 960, (k + 1) * 960); in every group of 8 consecutive devices one such range takes exactly 1024 from every device of the group. Padding positions carry ids too.
All inputs are finite; a program needn't handle non-finite values.
Results may differ from a plain program's by a relative error of at most 0.0029.
Values may be sent and summed in bfloat16 or wider, within the bound.
No kernel may reach another device: no remote copies, remote signals or barrier semaphores. Data moves between devices by JAX's collectives and lax.ppermute only.
A program may use at most 128 MiB of HBM per device.

v0:
```python
import jax
import jax.numpy as jnp
from jax import lax
from jax.sharding import PartitionSpec as P

VOCAB_DEV = 960
BLOCK = 128


def row_grads(grads, values, counts, gain):
    x = values.astype(jnp.float32)
    mu = jnp.mean(x, axis=1, keepdims=True)
    centered_input = x - mu
    inverse_deviation = lax.rsqrt(
        jnp.mean(centered_input * centered_input, axis=1, keepdims=True) + 1e-12
    )
    normalized_input = centered_input * inverse_deviation
    scaled_gradient = gain[None, :] * grads.astype(jnp.float32)
    first_term = jnp.mean(scaled_gradient, axis=1, keepdims=True)
    second_term = jnp.mean(scaled_gradient * normalized_input, axis=1, keepdims=True)
    input_gradient = inverse_deviation * (
        scaled_gradient - first_term - normalized_input * second_term
    )
    place = jnp.arange(x.shape[0], dtype=jnp.int32) % BLOCK
    alive = place < jnp.repeat(counts, BLOCK)
    return (jnp.where(alive[:, None], input_gradient, 0.0).astype(jnp.bfloat16), alive)


def per_device(token_ids, valid_counts, grad_output, pre_norm, norm_gain):
    tok_count = token_ids.shape[0]
    width = grad_output.shape[1]
    shards = lax.axis_size("vocab")
    per_owner = 2 * tok_count // shards
    rows, alive = row_grads(grad_output, pre_norm, valid_counts, norm_gain)
    owner = token_ids // VOCAB_DEV
    within = token_ids % VOCAB_DEV
    marks = (owner[:, None] == jnp.arange(shards, dtype=jnp.int32)[None, :]).astype(jnp.int32)
    rank = jnp.sum((jnp.cumsum(marks, axis=0) - 1) * marks, axis=1)
    target = owner * per_owner + rank
    outbox = jnp.zeros((shards * per_owner, width), jnp.bfloat16).at[target].set(rows)
    labels = (
        jnp.full((shards * per_owner,), -1, jnp.int32).at[target].set(jnp.where(alive, within, -1))
    )
    outbox = outbox.reshape(shards, per_owner, width)
    labels = labels.reshape(shards, per_owner)
    inlabels = lax.all_to_all(labels, "vocab", split_axis=0, concat_axis=0, tiled=True).reshape(
        shards * per_owner
    )
    picker = (jnp.arange(VOCAB_DEV, dtype=jnp.int32)[:, None] == inlabels[None, :]).astype(
        jnp.bfloat16
    )
    piece = lax.all_to_all(outbox, "vocab", split_axis=0, concat_axis=0, tiled=True)
    flat = piece.reshape(piece.shape[0] * piece.shape[1], piece.shape[2])
    partial_table = jnp.dot(picker, flat, preferred_element_type=jnp.float32)
    table = lax.psum(partial_table, "dp")
    return table


def solution(mesh):
    in_specs = (
        P(("dp", "vocab")),
        P(("dp", "vocab")),
        P(("dp", "vocab"), None),
        P(("dp", "vocab"), None),
        P(),
    )
    out_specs = P("vocab", None)
    return jax.shard_map(
        per_device, mesh=mesh, in_specs=in_specs, out_specs=out_specs, check_vma=False
    )
```

profile of v0, /device:TPU:0, one launch (start us, length us, event | category | flops | bytes accessed | tf_op | source)
XLA Modules:
  0.0 463.4 jit_solution(11556045148350424511)
XLA Ops:
  6.5 0.7 add_select_fusion.2
  7.3 2.3 reduce-window.6
  9.6 0.3 slice_reduce_fusion
  9.9 0.2 reduce-window.9
  10.1 0.1 add_bitcast_fusion
  10.2 0.1 fusion.24
  10.3 0.8 fusion.27
  11.1 16.1 %scatter_custom_fusion = s32[8192]{0:T(1024)} fusion(s32[4096]{0:T(1024)S(1)} %get-tuple-element.8, s32[4096]{0:T(1024)S(1)} %get-tuple-element.7, s32[]{:T(128)} %constant.49.clone.1), kind=kCustom, calls=%fused_computation.47 | custom fusion | bytes 32772 | tf_op jit(solution)/shard_map/scatter | solution.py:42
  27.2 6.4 %all-to-all-start = ((s32[8,1,1024]{2,1,0:T(1,128)}), s32[8,1,1024]{2,1,0:T(1,128)S(1)}, u32[]{:S(2)}, u32[]{:S(2)}) async-start(s32[8,1,1024]{2,1,0:T(1,128)} %bitcast.3), calls=%async_computation | async-start | bytes 65536 | tf_op jit(solution)/shard_map/all_to_all | solution.py:46
  33.6 0.0 all-reduce.2.cloned.1.call-start
  33.6 0.0 copy-start
  33.7 0.0 copy-start.1
  33.7 3.8 convert_reduce_fusion
  37.5 5.4 %fusion.11 = f32[4096]{0:T(1024)S(1)} fusion(bf16[4096,768]{1,0:T(8,128)(2,1)} %param.8, f32[4096]{0:T(1024)S(1)} %broadcast_multiply_fusion.2), kind=kLoop, calls=%fused_computation.16 | loop fusion | flops 12578816 | bytes 6324224 | tf_op jit(solution)/shard_map/reduce_sum | solution.py:15
  43.0 0.0 copy-done.2
  43.0 4.7 %fusion.12 = (f32[4096]{0:T(1024)S(1)}, f32[4096]{0:T(1024)S(1)}) fusion(bf16[4096,768]{1,0:T(8,128)(2,1)S(1)} %copy-done.1, f32[768]{0:T(1024)S(1)} %copy-done.2, f32[4096]{0:T(1024)S(1)} %add_rsqrt_fusion, f32[4096]{0:T(1024)S(1)} %broadcast_multiply_fusion.2, bf16[4096,768]{1,0:T(8,128)(2,1)S(1)} %copy-done), kind=kLoop, calls=%fused_computation.18 | loop fusion | flops 25157632 | bytes 12651520 | tf_op jit(solution)/shard_map/reduce_sum | solution.py:19
  47.7 0.1 fusion.26
  47.8 28.5 %scatter_custom_fusion.1 = bf16[8192,768]{1,0:T(8,128)(2,1)} fusion(s32[4096]{0:T(1024)S(1)} %get-tuple-element.8, bf16[4096,768]{1,0:T(8,128)(2,1)} %param.8, bf16[4096,768]{1,0:T(8,128)(2,1)} %param.7, f32[]{:T(128)} %constant.58.clone.1, f32[4096]{0:T(1024)S(1)} %get-tuple-element.11, f32[4096]{0:T(1024)S(1)} %get-tuple-element.12, ...), kind=kCustom, calls=%fused_computation.19 | custom fusion | flops 31457280 | bytes 25239558 | tf_op jit(solution)/shard_map/scatter | solution.py:40
  76.2 0.0 all-to-all-done
  76.2 278.8 %all_to_all.14 = bf16[8,1024,768]{2,1,0:T(8,128)(2,1)S(1)} all-to-all(bf16[8,1024,768]{2,1,0:T(8,128)(2,1)} %bitcast.28), channel_id=1, replica_groups=mesh['dp'=4,'vocab'=8] {'vocab'}, dimensions={0} | all-to-all | bytes 25165824 | tf_op jit(solution)/shard_map/all_to_all | solution.py:52
  355.0 15.1 %fusion = f32[960,768]{1,0:T(8,128)} fusion(bf16[8192,768]{1,0:T(8,128)(2,1)S(1)} %bitcast.29, s32[8192]{0:T(1024)S(1)} %bitcast.30), kind=kOutput, calls=%fused_computation.3 | convolution fusion | flops 12087459840 | bytes 15564800 | tf_op jit(solution)/shard_map/dot_general | solution.py:54
  370.1 0.0 all-reduce.2.cloned.1.call-update
  370.1 82.8 %all-reduce.2.cloned.1.call-done = f32[960,768]{1,0:T(8,128)} async-done(((f32[960,768]{1,0:T(8,128)}), f32[960,768]{1,0:T(8,128)}) %all-reduce.2.cloned.1.call-update) | async-done | bytes 2949136 | tf_op jit(solution)/shard_map/psum | solution.py:55
  452.9 3.6 copy.9
  (9 shorter events, 0.0 us)
Async XLA Ops:
  6.5 36.4 %copy-start.2 = (f32[768]{0:T(1024)S(1)}, f32[768]{0:T(1024)}, u32[]{:S(2)}) copy-start(f32[768]{0:T(1024)} %param.9) | copy-start | bytes 9220
  27.2 49.0 %all-to-all-start = ((s32[8,1,1024]{2,1,0:T(1,128)}), s32[8,1,1024]{2,1,0:T(1,128)S(1)}, u32[]{:S(2)}, u32[]{:S(2)}) async-start(s32[8,1,1024]{2,1,0:T(1,128)} %bitcast.3), calls=%async_computation | async-start | bytes 65536 | tf_op jit(solution)/shard_map/all_to_all | solution.py:46
  33.6 14.1 %copy-start.3 = (s32[32]{0:T(128)S(1)}, s32[32]{0:T(128)}, u32[]{:S(2)}) copy-start(s32[32]{0:T(128)} %param.6) | copy-start | bytes 388
  33.6 419.3 %all-reduce.2.cloned.1.call-start = ((), (), s32[]{:S(2)}) async-start(), calls=%async_computation.2 | async-start | bytes 5898240 | tf_op jit(solution)/shard_map/psum | solution.py:55
  33.6 9.3 %copy-start = (bf16[4096,768]{1,0:T(8,128)(2,1)S(1)}, bf16[4096,768]{1,0:T(8,128)(2,1)}, u32[]{:S(2)}) copy-start(bf16[4096,768]{1,0:T(8,128)(2,1)} %param.8) | copy-start | bytes 18874372
  33.7 9.3 %copy-start.1 = (bf16[4096,768]{1,0:T(8,128)(2,1)S(1)}, bf16[4096,768]{1,0:T(8,128)(2,1)}, u32[]{:S(2)}) copy-start(bf16[4096,768]{1,0:T(8,128)(2,1)} %param.7) | copy-start | bytes 18874372
Sparse Core Ops, SparseCore 0:
  370.3 82.5 all-reduce.1
where the time goes:
time: 464 us; the launch traced here: 463 us
  blocking collectives  279 us (60%)
  waiting for transfers between devices  82.8 us (18%)
  other arithmetic  46.7 us (10%)
  local copies, waits for them, and re-layouts  20 us (4%)
  matrix products  15.1 us (3%)
  between operations  13.5 us (3%)
  starting transfers between devices  6.39 us (1%)
    all_to_all x1, blocking collectives, per_device(): lax.all_to_all(outbox, 'vocab', split_axis=0, concat_axis=0, tiled=True)  279 us
    psum x1, waiting for transfers between devices, per_device(): table = lax.psum(partial_table, 'dp')  82.8 us
    scatter x1, other arithmetic, per_device(): jnp.zeros((shards * per_owner, width), jnp.bfloat16).at[target].set(rows)  28.5 us
    scatter x1, local copies, waits for them, and re-layouts, per_device(): jnp.full((shards * per_owner,), -1, jnp.int32).at[target]  16.1 us
    dot_general x1, matrix products, per_device(): partial_table = jnp.dot(picker, flat, preferred_element_type=jnp.float32)  15.1 us
  transfers between devices with their start and end apart: 2, of which 1 were waited for; matrix products, arithmetic and copies ran while one was open for 9% of the time, Pallas kernels for 0%

commit v1 on v0

--- a/solution.py
+++ b/solution.py
@@ -1,3 +1,4 @@
+import functools
 import jax
 import jax.numpy as jnp
 from jax import lax
@@ -5,6 +6,21 @@
 
 VOCAB_DEV = 960
 BLOCK = 128
+
+
+def wrap_pipes(z_in, peer_axis):
+    n_parts = lax.axis_size(peer_axis)
+    response = z_in
+    for q in [k0 for k0 in (1, 2, 4, 8, 16) if k0 < n_parts]:
+        slots = []
+        for u in range(n_parts):
+            slots.append((u, u ^ q))
+        moved = lax.ppermute(response, peer_axis, slots)
+        response = response + moved
+    return response
+
+
+_take_sheets = functools.partial(wrap_pipes, peer_axis="dp")
 
 
 def row_grads(grads, values, counts, gain):
@@ -52,7 +68,7 @@
     piece = lax.all_to_all(outbox, "vocab", split_axis=0, concat_axis=0, tiled=True)
     flat = piece.reshape(piece.shape[0] * piece.shape[1], piece.shape[2])
     partial_table = jnp.dot(picker, flat, preferred_element_type=jnp.float32)
-    table = lax.psum(partial_table, "dp")
+    table = _take_sheets(partial_table)
     return table
 
 

time: 464 us -> 495 us (1.067)
  waiting for transfers between devices: 82.8 us -> 127 us
  between operations: 13.5 us -> 0.15 us
    ppermute x0 -> x2, waiting for transfers between devices: none -> 127 us  [wrap_pipes(): moved = lax.ppermute(response, peer_axis, slots)]
    psum x1 -> x0, waiting for transfers between devices: 82.8 us -> none  [per_device(): table = lax.psum(partial_table, 'dp')]
  transfers between devices with their start and end apart: 2 -> 3, of which waited for: 1 -> 2; matrix products, arithmetic and copies ran while one was open for 9% -> 9% of each run, Pallas kernels for 0% -> 0%
where the time goes in v1:
time: 495 us; the launch traced here: 494 us
  blocking collectives  279 us (56%)
  waiting for transfers between devices  127 us (26%)
  other arithmetic  49.3 us (10%)
  local copies, waits for them, and re-layouts  16.4 us (3%)
  matrix products  13.5 us (3%)
  starting transfers between devices  9.5 us (2%)
    all_to_all x1, blocking collectives, per_device(): lax.all_to_all(outbox, 'vocab', split_axis=0, concat_axis=0, tiled=True)  279 us
    ppermute x2, waiting for transfers between devices, wrap_pipes(): moved = lax.ppermute(response, peer_axis, slots)  127 us
    scatter x1, other arithmetic, per_device(): jnp.zeros((shards * per_owner, width), jnp.bfloat16).at[target].set(rows)  28.5 us
    scatter x1, local copies, waits for them, and re-layouts, per_device(): jnp.full((shards * per_owner,), -1, jnp.int32).at[target]  16.1 us
    dot_general x1, matrix products, per_device(): partial_table = jnp.dot(picker, flat, preferred_element_type=jnp.float32)  13.5 us
  transfers between devices with their start and end apart: 3, of which 2 were waited for; matrix products, arithmetic and copies ran while one was open for 9% of the time, Pallas kernels for 0%

profile of v1, /device:TPU:0, one launch (start us, length us, event | category | flops | bytes accessed | tf_op | source)
XLA Modules:
  0.0 494.3 jit_solution(9127191938103784522)
XLA Ops:
  0.0 0.9 add_select_fusion.2
  0.9 2.3 reduce-window.6
  3.2 0.3 slice_reduce_fusion
  3.5 0.2 reduce-window.9
  3.7 0.1 add_bitcast_fusion
  3.8 0.1 fusion.24
  4.0 0.8 fusion.27
  4.7 16.1 %scatter_custom_fusion = s32[8192]{0:T(1024)} fusion(s32[4096]{0:T(1024)S(1)} %get-tuple-element.8, s32[4096]{0:T(1024)S(1)} %get-tuple-element.7, s32[]{:T(128)} %constant.49.clone.1), kind=kCustom, calls=%fused_computation.47 | custom fusion | bytes 32772 | tf_op jit(solution)/shard_map/scatter | solution.py:58
  20.8 6.4 %all-to-all-start = ((s32[8,1,1024]{2,1,0:T(1,128)}), s32[8,1,1024]{2,1,0:T(1,128)S(1)}, u32[]{:S(2)}, u32[]{:S(2)}) async-start(s32[8,1,1024]{2,1,0:T(1,128)} %bitcast.3), calls=%async_computation | async-start | bytes 65536 | tf_op jit(solution)/shard_map/all_to_all | solution.py:62
  27.2 0.0 copy-start
  27.2 0.0 copy-start.2
  27.2 3.8 convert_reduce_fusion
  31.1 5.5 %fusion.11 = f32[4096]{0:T(1024)S(1)} fusion(bf16[4096,768]{1,0:T(8,128)(2,1)} %param.8, f32[4096]{0:T(1024)S(1)} %broadcast_multiply_fusion.2), kind=kLoop, calls=%fused_computation.16 | loop fusion | flops 12578816 | bytes 6324224 | tf_op jit(solution)/shard_map/reduce_sum | solution.py:31
  36.6 4.7 fusion.12
  41.3 0.1 fusion.26
  41.4 28.5 %scatter_custom_fusion.1 = bf16[8192,768]{1,0:T(8,128)(2,1)} fusion(s32[4096]{0:T(1024)S(1)} %get-tuple-element.8, bf16[4096,768]{1,0:T(8,128)(2,1)} %param.8, bf16[4096,768]{1,0:T(8,128)(2,1)} %param.7, f32[]{:T(128)} %constant.58.clone.1, f32[4096]{0:T(1024)S(1)} %get-tuple-element.11, f32[4096]{0:T(1024)S(1)} %get-tuple-element.12, ...), kind=kCustom, calls=%fused_computation.19 | custom fusion | flops 31457280 | bytes 25239558 | tf_op jit(solution)/shard_map/scatter | solution.py:56
  69.8 278.8 %all_to_all.14 = bf16[8,1024,768]{2,1,0:T(8,128)(2,1)S(1)} all-to-all(bf16[8,1024,768]{2,1,0:T(8,128)(2,1)} %bitcast.30), channel_id=1, replica_groups=mesh['dp'=4,'vocab'=8] {'vocab'}, dimensions={0} | all-to-all | bytes 25165824 | tf_op jit(solution)/shard_map/all_to_all | solution.py:68
  348.7 13.5 %fusion = f32[960,768]{1,0:T(8,128)S(1)} fusion(bf16[8192,768]{1,0:T(8,128)(2,1)S(1)} %bitcast.31, s32[8192]{0:T(1024)S(1)} %bitcast.32), kind=kOutput, calls=%fused_computation.3 | convolution fusion | flops 12087459840 | bytes 15564800 | tf_op jit(solution)/shard_map/dot_general | solution.py:70
  362.2 1.6 collective-permute-start
  363.7 63.8 %collective-permute-done = f32[960,768]{1,0:T(8,128)S(1)} collective-permute-done((f32[960,768]{1,0:T(8,128)S(1)}, f32[960,768]{1,0:T(8,128)S(1)}, u32[]{:S(2)}, u32[]{:S(2)}) %collective-permute-start) | collective-permute-done | bytes 2949152 | tf_op jit(solution)/shard_map/ppermute | solution.py:18
  427.5 0.4 add.48
  427.9 1.6 collective-permute-start.1
  429.5 62.9 %collective-permute-done.1 = f32[960,768]{1,0:T(8,128)S(1)} collective-permute-done((f32[960,768]{1,0:T(8,128)S(1)}, f32[960,768]{1,0:T(8,128)S(1)}, u32[]{:S(2)}, u32[]{:S(2)}) %collective-permute-start.1) | collective-permute-done | bytes 2949152 | tf_op jit(solution)/shard_map/ppermute | solution.py:18
  492.4 2.0 add.49
  (14 shorter events, 0.0 us)
Async XLA Ops:
  0.0 36.6 %slice-start = ((s8[6291456]{0:T(1024)(128)(4,1)}), s8[2097152]{0:T(1024)(128)(4,1)S(1)}, s32[]{:S(2)}) async-start(s8[6291456]{0:T(1024)(128)(4,1)} %bitcast.28), calls=%async_computation.2 | async-start | bytes 4194304
  0.0 36.6 %copy-start.1 = (f32[768]{0:T(1024)S(1)}, f32[768]{0:T(1024)}, u32[]{:S(2)}) copy-start(f32[768]{0:T(1024)} %param.9) | copy-start | bytes 9220
  20.8 49.0 %all-to-all-start = ((s32[8,1,1024]{2,1,0:T(1,128)}), s32[8,1,1024]{2,1,0:T(1,128)S(1)}, u32[]{:S(2)}, u32[]{:S(2)}) async-start(s32[8,1,1024]{2,1,0:T(1,128)} %bitcast.3), calls=%async_computation | async-start | bytes 65536 | tf_op jit(solution)/shard_map/all_to_all | solution.py:62
  27.2 9.4 %slice-start.1 = ((s8[6291456]{0:T(1024)(128)(4,1)}), s8[4194304]{0:T(1024)(128)(4,1)S(1)}, s32[]{:S(2)}) async-start(s8[6291456]{0:T(1024)(128)(4,1)} %bitcast.28), calls=%async_computation.3 | async-start | bytes 8388608
  27.2 9.4 %copy-start = (bf16[4096,768]{1,0:T(8,128)(2,1)S(1)}, bf16[4096,768]{1,0:T(8,128)(2,1)}, u32[]{:S(2)}) copy-start(bf16[4096,768]{1,0:T(8,128)(2,1)} %param.7) | copy-start | bytes 18874372
  27.2 14.1 %copy-start.2 = (s32[32]{0:T(128)S(1)}, s32[32]{0:T(128)}, u32[]{:S(2)}) copy-start(s32[32]{0:T(128)} %param.6) | copy-start | bytes 388
  362.2 65.3 %collective-permute-start = (f32[960,768]{1,0:T(8,128)S(1)}, f32[960,768]{1,0:T(8,128)S(1)}, u32[]{:S(2)}, u32[]{:S(2)}) collective-permute-start(f32[960,768]{1,0:T(8,128)S(1)} %fusion), channel_id=1, source_target_pairs={{0,8},{8,0},{16,24},{24,16},{1,9},{9,1},{17,25},{25,17},{2,10},{10... | collective-permute-start | bytes 8847368 | tf_op jit(solution)/shard_map/ppermute | solution.py:18
  427.9 64.5 %collective-permute-start.1 = (f32[960,768]{1,0:T(8,128)S(1)}, f32[960,768]{1,0:T(8,128)S(1)}, u32[]{:S(2)}, u32[]{:S(2)}) collective-permute-start(f32[960,768]{1,0:T(8,128)S(1)} %add.48), channel_id=1, source_target_pairs={{0,16},{8,24},{16,0},{24,8},{1,17},{9,25},{17,1},{25,9},{2,18},{10... | collective-permute-start | bytes 8847368 | tf_op jit(solution)/shard_map/ppermute | solution.py:18
